TPU v7x, 16 devices: a whole 2x2x2 slice. The times are simulated.
16 devices in a mesh: dp: 4 (over z, y), sp: 4 (over x, core).
Axes of the slice: x: 2, y: 2, z: 2, core: 2. Of those that a mesh axis runs over, the one named last changes fastest.
Arguments:
- hidden: bfloat16 [32, 768, 3072], P('dp', 'sp'), parts along dimension 0
- cond_vec: bfloat16 [32, 3072], P('dp'), parts along dimension 0
- pos_ids: int32 [768, 3], P('sp')
- w_mod: bfloat16 [2, 3072, 9216], replicated
- b_mod: bfloat16 [2, 9216], replicated
- w_in: bfloat16 [2, 3072, 21504], replicated
- b_in: bfloat16 [2, 21504], replicated
- q_gain: bfloat16 [2, 128], replicated
- k_gain: bfloat16 [2, 128], replicated
- w_out: bfloat16 [2, 15360, 3072], replicated
- b_out: bfloat16 [2, 3072], replicated
Outputs:
- output: bfloat16 [32, 768, 3072], P('dp', 'sp'), parts along dimension 0
There are 4 independent parts. A program takes and returns all parts, laid end to end along the dimension named above; an argument that names none is the same for every part.
All inputs are finite; a program needn't handle non-finite values.
Results may differ from a plain program's by a relative error of at most 0.0115895.
Values are sent between devices in bfloat16 or wider.
A program may use at most 2.25 GiB of HBM per device.

v0:
```python
import math
import jax
import jax.numpy as jnp
from jax import lax
from jax.sharding import PartitionSpec as P

HEAD = 128
ROPE_SPLIT = (16, 56, 56)
ROPE_THETA = 10000.0
NORM_EPS = 1e-6
Q_BLOCK = 256


def rope_tables(pos_ids):
    angle_parts = []
    for column, rope_dim in enumerate(ROPE_SPLIT):
        inv_freq = 1.0 / (ROPE_THETA ** (jnp.arange(0, rope_dim, 2, dtype=jnp.float32) / rope_dim))
        angle_parts.append(pos_ids[:, column:column + 1].astype(jnp.float32) * inv_freq)
    angles = jnp.concatenate(angle_parts, axis=1)
    return jnp.cos(angles), jnp.sin(angles)


def rms_norm(tensor, gain):
    sq_mean = jnp.mean(tensor * tensor, axis=-1, keepdims=True)
    return tensor * lax.rsqrt(sq_mean + NORM_EPS) * gain.astype(jnp.float32)


def apply_rope(tensor, cos_t, sin_t):
    paired = tensor.reshape(tensor.shape[:-1] + (tensor.shape[-1] // 2, 2))
    even_v = paired[..., 0]
    odd_v = paired[..., 1]
    cos_b = cos_t[None, :, None, :]
    sin_b = sin_t[None, :, None, :]
    rotated = jnp.stack([even_v * cos_b - odd_v * sin_b, even_v * sin_b + odd_v * cos_b], axis=-1)
    return rotated.reshape(tensor.shape)


def modulation(cond_vec, w_mod, b_mod):
    mod_act = jax.nn.silu(cond_vec.astype(jnp.float32)).astype(jnp.bfloat16)
    mod_vals = jnp.dot(mod_act, w_mod, preferred_element_type=jnp.float32) + b_mod.astype(jnp.float32)
    mod_vals = mod_vals.astype(jnp.bfloat16).astype(jnp.float32)
    return jnp.split(mod_vals[:, None, :], 3, axis=-1)


def project_in(hidden, mod_shift, mod_scale, w_in, b_in):
    x_float = hidden.astype(jnp.float32)
    centered = x_float - jnp.mean(x_float, axis=-1, keepdims=True)
    normed = centered * lax.rsqrt(jnp.mean(centered * centered, axis=-1, keepdims=True) + NORM_EPS)
    modded = ((1.0 + mod_scale) * normed + mod_shift).astype(jnp.bfloat16)
    proj_f = jnp.einsum('bsd,dn->bsn', modded, w_in, preferred_element_type=jnp.float32)
    return (proj_f + b_in.astype(jnp.float32)).astype(jnp.bfloat16)


def qkv_heads(proj_in, model_dim, q_gain, k_gain, cos_t, sin_t):
    head_shape = proj_in.shape[:2] + (model_dim // HEAD, HEAD)
    q_raw = proj_in[..., :model_dim].reshape(head_shape).astype(jnp.float32)
    k_raw = proj_in[..., model_dim:2 * model_dim].reshape(head_shape).astype(jnp.float32)
    v_heads = proj_in[..., 2 * model_dim:3 * model_dim].reshape(head_shape)
    q_heads = apply_rope(rms_norm(q_raw, q_gain), cos_t, sin_t).astype(jnp.bfloat16)
    k_heads = apply_rope(rms_norm(k_raw, k_gain), cos_t, sin_t).astype(jnp.bfloat16)
    return q_heads, k_heads, v_heads


def local_attention(queries, keys_all, values_all):
    n_batch, q_rows, n_heads, head_dim = queries.shape
    q_block = math.gcd(q_rows, Q_BLOCK)
    score_scale = head_dim ** -0.5

    def per_block(blk_idx):
        q_blk = lax.dynamic_slice_in_dim(queries, blk_idx * q_block, q_block, axis=1)
        scores = jnp.einsum('bqhd,bkhd->bhqk', q_blk, keys_all, preferred_element_type=jnp.float32) * score_scale
        row_max = jnp.max(scores, axis=-1, keepdims=True)
        weights = jnp.exp(scores - row_max)
        row_sum = jnp.sum(weights, axis=-1)
        attn_blk = jnp.einsum('bhqk,bkhd->bqhd', weights.astype(jnp.bfloat16), values_all, preferred_element_type=jnp.float32)
        return (attn_blk / jnp.swapaxes(row_sum, 1, 2)[..., None]).astype(jnp.bfloat16)

    blocks_out = lax.map(per_block, jnp.arange(q_rows // q_block))
    return jnp.moveaxis(blocks_out, 0, 1).reshape(n_batch, q_rows, n_heads, head_dim)


def project_out(hidden, attn_out, mlp_in, mod_gate, w_out, b_out):
    model_dim = attn_out.shape[-1]
    mlp_act = jax.nn.gelu(mlp_in.astype(jnp.float32), approximate=True).astype(jnp.bfloat16)
    out_f = jnp.einsum('bsd,dn->bsn', attn_out, w_out[:model_dim], preferred_element_type=jnp.float32)
    out_f = out_f + jnp.einsum('bsm,mn->bsn', mlp_act, w_out[model_dim:], preferred_element_type=jnp.float32)
    block_out = (out_f + b_out.astype(jnp.float32)).astype(jnp.bfloat16)
    return (hidden.astype(jnp.float32) + mod_gate * block_out.astype(jnp.float32)).astype(jnp.bfloat16)


def solution(mesh):
    row_spec = P('dp', 'sp', None)
    replicated = P()

    def local_forward(hidden, cond_vec, pos_ids, w_mod, b_mod, w_in, b_in, q_gain, k_gain, w_out, b_out):
        cos_t, sin_t = rope_tables(pos_ids)
        n_batch, local_rows, model_dim = hidden.shape
        for layer_idx in range(w_mod.shape[0]):
            mod_shift, mod_scale, mod_gate = modulation(cond_vec, w_mod[layer_idx], b_mod[layer_idx])
            proj_in = project_in(hidden, mod_shift, mod_scale, w_in[layer_idx], b_in[layer_idx])
            q_heads, k_heads, v_heads = qkv_heads(proj_in, model_dim, q_gain[layer_idx], k_gain[layer_idx], cos_t, sin_t)
            q_seq = lax.all_to_all(q_heads, 'sp', 2, 1, tiled=True)
            k_seq = lax.all_to_all(k_heads, 'sp', 2, 1, tiled=True)
            v_seq = lax.all_to_all(v_heads, 'sp', 2, 1, tiled=True)
            attn_seq = local_attention(q_seq, k_seq, v_seq)
            attn_rows = lax.all_to_all(attn_seq, 'sp', 1, 2, tiled=True).reshape(n_batch, local_rows, model_dim)
            hidden = project_out(hidden, attn_rows, proj_in[..., 3 * model_dim:], mod_gate, w_out[layer_idx], b_out[layer_idx])
        return hidden

    in_specs = (row_spec, P('dp', None), P('sp', None), replicated, replicated, replicated, replicated, replicated, replicated, replicated, replicated)
    return jax.shard_map(local_forward, mesh=mesh, in_specs=in_specs, out_specs=row_spec, check_vma=False)
```

profile of v0, /device:TPU:0, one launch (start us, length us, event | category | flops | bytes accessed | tf_op | source)
XLA Modules:
  0.0 2466.9 jit_solution(14319738038942455207)
XLA Ops:
  12.7 20.0 fusion.105
  46.7 217.6 %add_convert_fusion.1 = bf16[8,192,21504]{2,1,0:T(8,128)(2,1)} fusion(f32[21504]{0:T(1024)S(1)} %bitcast.265, bf16[2,3072,21504]{2,1,0:T(8,128)(2,1)} %param.20, bf16[8,192,3072]{2,1,0:T(8,128)(2,1)} %fusion.180), kind=kOutput, calls=%fused_computation.42 | convolution fusion | flops 203003265024 | bytes 207704064 | tf_op jit(solution)/shard_map/bsd,dn->bsn/dot_general | solution.py:50
  264.3 25.7 %slice_bitcast_fusion.1 = (bf16[8,24,24,8,128]{4,3,2,1,0:T(8,128)(2,1)}, f32[8,192,3072]{2,1,0:T(8,128)}, f32[8,192,3072]{2,1,0:T(8,128)}) fusion(bf16[8,192,21504]{2,1,0:T(8,128)(2,1)} %add_convert_fusion.1), kind=kLoop, calls=%fused_computation.137 | loop fusion | flops 9437184 | bytes 75497472
  305.9 19.4 fusion.133
  358.2 25.0 %copy.139 = f32[8,192,3072]{1,0,2:T(8,128)} copy(f32[8,192,3072]{2,1,0:T(8,128)} %get-tuple-element.109) | data formatting | bytes 37748736 | tf_op jit(solution)/shard_map/convert_element_type | solution.py:57
  383.2 24.9 %copy.132 = f32[8,192,3072]{1,0,2:T(8,128)} copy(f32[8,192,3072]{2,1,0:T(8,128)} %get-tuple-element.110) | data formatting | bytes 37748736 | tf_op jit(solution)/shard_map/convert_element_type | solution.py:56
  408.6 19.0 multiply_multiply_fusion.2
  441.4 27.3 %subtract_convert_fusion.2 = (bf16[8,192,24,64,1]{1,0,4,3,2:T(8,128)(2,1)}, bf16[8,192,24,64,1]{1,0,4,3,2:T(8,128)(2,1)}, bf16[8,192,24,64,1]{1,0,4,3,2:T(8,128)(2,1)}, bf16[8,192,24,64,1]{1,0,4,3,2:T(8,128)(2,1)}) fusion(f32[8,192,24,64,2]{1,0,4,3,2:T(8,128)} %multiply_multiply_fusion.2, f32[192,64]{0,1:T(8,128)S(1)} %get-tuple-element.134, ...), kind=kLoop, calls=%fused_computation.121 | loop fusion | flops 37748736 | bytes 56721408 | tf_op jit(solution)/shard_map/convert.20
  528.4 78.0 %all-to-all-done.1 = bf16[8,192,24,128]{3,1,0,2:T(8,128)(2,1)} async-done(((bf16[8,192,24,128]{3,1,0,2:T(8,128)(2,1)}), bf16[8,192,24,128]{3,1,0,2:T(8,128)(2,1)}, u32[]{:S(2)}, u32[]{:S(2)}) %all-to-all-start.1) | async-done | bytes 9437216 | tf_op jit(solution)/shard_map/all_to_all | solution.py:103
  632.6 83.7 %all-to-all-done = bf16[8,192,24,128]{3,1,0,2:T(8,128)(2,1)} async-done(((bf16[8,192,24,128]{3,1,0,2:T(8,128)(2,1)}), bf16[8,192,24,128]{3,1,0,2:T(8,128)(2,1)}, u32[]{:S(2)}, u32[]{:S(2)}) %all-to-all-start) | async-done | bytes 9437216 | tf_op jit(solution)/shard_map/all_to_all | solution.py:102
  732.7 163.1 %while.20 = (s32[]{:T(128)}, bf16[3,8,256,6,128]{4,2,0,3,1:T(8,128)(2,1)}, s32[3]{0:T(128)S(1)}, bf16[8,768,6,128]{3,1,2,0:T(8,128)(2,1)}, bf16[8,768,6,128]{3,1...) while((s32[]{:T(128)}, ...), condition=%wide.region_7.8_spmd, body=%wide.region_4.7_spmd.sunk | while | flops 4910456832 | bytes 176406736 | solution.py:78
  734.0 17.6 multiply_reduce_fusion.4
  751.6 18.2 fusion.193
  769.9 17.2 bitcast_dynamic-update-slice_fusion.4
  788.2 17.6 multiply_reduce_fusion.4
  805.8 18.2 fusion.193
  824.0 17.2 bitcast_dynamic-update-slice_fusion.4
  842.4 17.6 multiply_reduce_fusion.4
  859.9 18.2 fusion.193
  878.2 17.2 bitcast_dynamic-update-slice_fusion.4
  917.4 19.9 fusion.111
  938.0 81.3 %all-to-all-done.3 = bf16[8,768,6,128]{3,0,2,1:T(8,128)(2,1)} async-done(((bf16[8,768,6,128]{3,0,2,1:T(8,128)(2,1)}), bf16[8,768,6,128]{3,0,2,1:T(8,128)(2,1)}, u32[]{:S(2)}, u32[]{:S(2)}) %all-to-all-start.3) | async-done | bytes 9437216 | tf_op jit(solution)/shard_map/all_to_all | solution.py:106
  1030.1 19.1 reshape.291
  1049.3 37.5 %fusion.86 = f32[8,192,3072]{2,1,0:T(8,128)} fusion(bf16[8,192,3072]{2,1,0:T(8,128)(2,1)} %reshape.291, bf16[2,15360,3072]{2,1,0:T(8,128)(2,1)} %param.24), kind=kOutput, calls=%fused_computation.106 | convolution fusion | flops 28991029248 | bytes 47185920 | tf_op jit(solution)/shard_map/bsd,dn->bsn/dot_general | solution.py:85
  1086.8 157.0 %convert_reduce_fusion = (f32[8,192]{1,0:T(8,128)S(1)}, bf16[8,192,3072]{2,1,0:T(8,128)(2,1)}) fusion(f32[3072]{0:T(1024)S(1)} %bitcast.267, f32[8,192,3072]{2,1,0:T(8,128)} %fusion.86, bf16[2,15360,3072]{2,1,0:T(8,128)(2,1)} %param.24, bf16[8,192,21504]{2,1,0:T(8,128)(2,1)} %add_convert_fusion.1, f32[8,3072]{1,0:T(8,128)S(1)} %copy-done.17, ...), kind=kOutput, calls=%fused_computation.78 | convolution fusion | flops 116200046592 | bytes 151111680 | tf_op jit(solution)/shard_map/bsm,mn->bsn/dot_general | solution.py:86
  1263.2 217.4 %add_convert_fusion = bf16[8,192,21504]{2,1,0:T(8,128)(2,1)} fusion(f32[21504]{0:T(1024)S(1)} %bitcast.264, bf16[2,3072,21504]{2,1,0:T(8,128)(2,1)} %param.20, bf16[8,192,3072]{2,1,0:T(8,128)(2,1)} %fusion.178), kind=kOutput, calls=%fused_computation.36 | convolution fusion | flops 203003265024 | bytes 207704064 | tf_op jit(solution)/shard_map/bsd,dn->bsn/dot_general | solution.py:50
  1496.8 25.5 %slice_bitcast_fusion = (bf16[8,24,24,8,128]{4,3,2,1,0:T(8,128)(2,1)}, f32[8,192,3072]{2,1,0:T(8,128)}, f32[8,192,3072]{2,1,0:T(8,128)}) fusion(bf16[8,192,21504]{2,1,0:T(8,128)(2,1)} %add_convert_fusion), kind=kLoop, calls=%fused_computation.134 | loop fusion | flops 9437184 | bytes 75497472
  1542.0 17.8 copy.198
  1587.8 24.9 %copy.160 = f32[8,192,3072]{1,0,2:T(8,128)} copy(f32[8,192,3072]{2,1,0:T(8,128)} %get-tuple-element.104) | data formatting | bytes 37748736 | tf_op jit(solution)/shard_map/convert_element_type | solution.py:57
  1612.8 24.9 %copy.153 = f32[8,192,3072]{1,0,2:T(8,128)} copy(f32[8,192,3072]{2,1,0:T(8,128)} %get-tuple-element.105) | data formatting | bytes 37748736 | tf_op jit(solution)/shard_map/convert_element_type | solution.py:56
  1637.7 20.4 multiply_multiply_fusion
  1670.6 27.0 %subtract_convert_fusion = (bf16[8,192,24,64,1]{1,0,4,3,2:T(8,128)(2,1)}, bf16[8,192,24,64,1]{1,0,4,3,2:T(8,128)(2,1)}, bf16[8,192,24,64,1]{1,0,4,3,2:T(8,128)(2,1)}, bf16[8,192,24,64,1]{1,0,4,3,2:T(8,128)(2,1)}) fusion(f32[8,192,24,64,2]{1,0,4,3,2:T(8,128)} %multiply_multiply_fusion, f32[192,64]{0,1:T(8,128)S(1)} %copy-done.7, f32[192,64]{0,1:T(8,128)S(1)} %copy-done.5, ...), kind=kLoop, calls=%fused_computation.117 | loop fusion | flops 37748736 | bytes 56721408 | tf_op jit(solution)/shard_map/convert.16
  1757.4 77.1 %all-to-all-done.5 = bf16[8,192,24,128]{3,1,0,2:T(8,128)(2,1)} async-done(((bf16[8,192,24,128]{3,1,0,2:T(8,128)(2,1)}), bf16[8,192,24,128]{3,1,0,2:T(8,128)(2,1)}, u32[]{:S(2)}, u32[]{:S(2)}) %all-to-all-start.5) | async-done | bytes 9437216 | tf_op jit(solution)/shard_map/all_to_all | solution.py:103
  1861.1 83.7 %all-to-all-done.4 = bf16[8,192,24,128]{3,1,0,2:T(8,128)(2,1)} async-done(((bf16[8,192,24,128]{3,1,0,2:T(8,128)(2,1)}), bf16[8,192,24,128]{3,1,0,2:T(8,128)(2,1)}, u32[]{:S(2)}, u32[]{:S(2)}) %all-to-all-start.4) | async-done | bytes 9437216 | tf_op jit(solution)/shard_map/all_to_all | solution.py:102
  1961.0 163.3 %while.21 = (s32[]{:T(128)}, bf16[3,8,256,6,128]{4,2,0,3,1:T(8,128)(2,1)}, s32[3]{0:T(128)S(1)}, bf16[8,768,6,128]{3,1,2,0:T(8,128)(2,1)}, bf16[8,768,6,128]{3,1...) while((s32[]{:T(128)}, ...), condition=%wide.region_15.16_spmd, body=%wide.region_12.15_spmd.sunk | while | flops 4910456832 | bytes 176406736 | solution.py:78
  1962.4 17.6 multiply_reduce_fusion.5
  1980.0 18.2 fusion.197
  1998.3 17.2 bitcast_dynamic-update-slice_fusion.5
  2016.8 17.6 multiply_reduce_fusion.5
  2034.4 18.2 fusion.197
  2052.6 17.2 bitcast_dynamic-update-slice_fusion.5
  2071.1 17.6 multiply_reduce_fusion.5
  2088.7 18.2 fusion.197
  2106.9 17.2 bitcast_dynamic-update-slice_fusion.5
  2137.6 108.5 %all_to_all.138 = bf16[8,768,6,128]{3,0,2,1:T(8,128)(2,1)S(1)} all-to-all(bf16[8,768,6,128]{3,0,2,1:T(8,128)(2,1)} %copy.171), channel_id=1, replica_groups=mesh['dp'=4,'sp'=4] {'sp'}, dimensions={1} | all-to-all | bytes 18874368 | tf_op jit(solution)/shard_map/all_to_all | solution.py:106
  2253.5 19.2 reshape.294
  2272.7 37.5 %fusion.84 = f32[8,192,3072]{2,1,0:T(8,128)} fusion(bf16[8,192,3072]{2,1,0:T(8,128)(2,1)} %reshape.294, bf16[2,15360,3072]{2,1,0:T(8,128)(2,1)} %param.24), kind=kOutput, calls=%fused_computation.104 | convolution fusion | flops 28991029248 | bytes 47185920 | tf_op jit(solution)/shard_map/bsd,dn->bsn/dot_general | solution.py:85
  2310.3 156.3 %fusion.83 = bf16[8,192,3072]{2,1,0:T(8,128)(2,1)} fusion(bf16[8,192,3072]{2,1,0:T(8,128)(2,1)} %get-tuple-element.145, f32[8,192,3072]{2,1,0:T(8,128)} %fusion.84, f32[3072]{0:T(1024)S(1)} %bitcast.266, f32[8,3072]{1,0:T(8,128)S(1)} %copy-done.18, bf16[2,15360,3072]{2,1,0:T(8,128)(2,1)} %param.24, bf16[8,192,21504]{2,1,0:T(8,128)(2,1)} %add_convert_fusion), kind=kOutput, calls=%fused_computation.99 | convolution fusion | flops 116190609408 | bytes 151105536 | tf_op jit(solution)/shard_map/bsm,mn->bsn/dot_general | solution.py:86
  (148 shorter events, 447.4 us)
Async XLA Ops:
  0.0 11.3 copy-start.14
  0.0 12.0 copy-start.10
  0.0 12.7 copy-start.11
  300.1 195.5 %all-to-all-start.2 = ((bf16[8,192,24,128]{3,1,0,2:T(8,128)(2,1)}), bf16[8,192,24,128]{3,1,0,2:T(8,128)(2,1)}, u32[]{:S(2)}, u32[]{:S(2)}) async-start(bf16[8,192,24,128]{3,1,0,2:T(8,128)(2,1)} %bitcast.253), calls=%async_computation.2 | async-start | bytes 18874368 | tf_op jit(solution)/shard_map/all_to_all | solution.py:104
  305.9 19.5 copy-start.25
  305.9 19.5 copy-start.26
  383.2 25.0 %copy-start.22 = (s32[192,3]{0,1:T(4,128)S(1)}, s32[192,3]{0,1:T(4,128)}, u32[]{:S(2)}) copy-start(s32[192,3]{0,1:T(4,128)} %param.17) | copy-start | bytes 6916
  408.5 32.9 %copy-start.4 = (f32[192,64]{0,1:T(8,128)}, f32[192,64]{0,1:T(8,128)S(1)}, u32[]{:S(2)}) copy-start(f32[192,64]{0,1:T(8,128)S(1)} %get-tuple-element.133) | copy-start | bytes 147460
  408.6 32.9 %copy-start.6 = (f32[192,64]{0,1:T(8,128)}, f32[192,64]{0,1:T(8,128)S(1)}, u32[]{:S(2)}) copy-start(f32[192,64]{0,1:T(8,128)S(1)} %get-tuple-element.134) | copy-start | bytes 147460
  408.6 24.2 copy-start
  495.6 110.8 %all-to-all-start.1 = ((bf16[8,192,24,128]{3,1,0,2:T(8,128)(2,1)}), bf16[8,192,24,128]{3,1,0,2:T(8,128)(2,1)}, u32[]{:S(2)}, u32[]{:S(2)}) async-start(bf16[8,192,24,128]{3,1,0,2:T(8,128)(2,1)} %copy.143), calls=%async_computation.1 | async-start | bytes 18874368 | tf_op jit(solution)/shard_map/all_to_all | solution.py:103
  606.5 109.9 %all-to-all-start = ((bf16[8,192,24,128]{3,1,0,2:T(8,128)(2,1)}), bf16[8,192,24,128]{3,1,0,2:T(8,128)(2,1)}, u32[]{:S(2)}, u32[]{:S(2)}) async-start(bf16[8,192,24,128]{3,1,0,2:T(8,128)(2,1)} %copy.136), calls=%async_computation | async-start | bytes 18874368 | tf_op jit(solution)/shard_map/all_to_all | solution.py:102
  751.6 18.2 copy-start.3
  805.8 18.2 copy-start.3
  859.9 18.2 copy-start.3
  895.8 19.5 copy-start.24
  895.8 20.3 copy-start.23
  895.8 21.0 copy-start.20
  895.8 21.6 copy-start.12
  895.8 21.6 copy-start.13
  909.1 110.2 %all-to-all-start.3 = ((bf16[8,768,6,128]{3,0,2,1:T(8,128)(2,1)}), bf16[8,768,6,128]{3,0,2,1:T(8,128)(2,1)}, u32[]{:S(2)}, u32[]{:S(2)}) async-start(bf16[8,768,6,128]{3,0,2,1:T(8,128)(2,1)} %copy.150), calls=%async_computation.3 | async-start | bytes 18874368 | tf_op jit(solution)/shard_map/all_to_all | solution.py:106
  1049.3 37.5 %copy-start.17 = (f32[8,3072]{1,0:T(8,128)S(1)}, f32[8,3072]{1,0:T(8,128)}, u32[]{:S(2)}) copy-start(f32[8,3072]{1,0:T(8,128)} %get-tuple-element.124) | copy-start | bytes 294916
  1086.8 163.4 %copy-start.8 = (f32[8,3072]{1,0:T(8,128)S(1)}, f32[8,3072]{1,0:T(8,128)}, u32[]{:S(2)}) copy-start(f32[8,3072]{1,0:T(8,128)} %get-tuple-element.122) | copy-start | bytes 294916
  1086.8 163.4 %copy-start.9 = (f32[8,3072]{1,0:T(8,128)S(1)}, f32[8,3072]{1,0:T(8,128)}, u32[]{:S(2)}) copy-start(f32[8,3072]{1,0:T(8,128)} %get-tuple-element.123) | copy-start | bytes 294916
  1243.8 19.4 copy-start.19
  1570.0 154.5 %all-to-all-start.6 = ((bf16[8,192,24,128]{3,1,0,2:T(8,128)(2,1)}), bf16[8,192,24,128]{3,1,0,2:T(8,128)(2,1)}, u32[]{:S(2)}, u32[]{:S(2)}) async-start(bf16[8,192,24,128]{3,1,0,2:T(8,128)(2,1)} %bitcast.254), calls=%async_computation.6 | async-start | bytes 18874368 | tf_op jit(solution)/shard_map/all_to_all | solution.py:104
  1612.8 24.9 %copy-start.16 = (f32[64,2]{1,0:T(8,128)S(1)}, f32[64,2]{1,0:T(8,128)}, u32[]{:S(2)}) copy-start(f32[64,2]{1,0:T(8,128)} %reshape.309) | copy-start | bytes 1540
  1637.7 24.1 copy-start.1
  1637.7 24.1 copy-start.15
  1661.8 8.7 copy-start.5
  1661.8 8.7 copy-start.7
  1724.4 110.0 %all-to-all-start.5 = ((bf16[8,192,24,128]{3,1,0,2:T(8,128)(2,1)}), bf16[8,192,24,128]{3,1,0,2:T(8,128)(2,1)}, u32[]{:S(2)}, u32[]{:S(2)}) async-start(bf16[8,192,24,128]{3,1,0,2:T(8,128)(2,1)} %copy.164), calls=%async_computation.5 | async-start | bytes 18874368 | tf_op jit(solution)/shard_map/all_to_all | solution.py:103
  1834.5 110.3 %all-to-all-start.4 = ((bf16[8,192,24,128]{3,1,0,2:T(8,128)(2,1)}), bf16[8,192,24,128]{3,1,0,2:T(8,128)(2,1)}, u32[]{:S(2)}, u32[]{:S(2)}) async-start(bf16[8,192,24,128]{3,1,0,2:T(8,128)(2,1)} %copy.157), calls=%async_computation.4 | async-start | bytes 18874368 | tf_op jit(solution)/shard_map/all_to_all | solution.py:102
  1980.0 18.2 copy-start.2
  2034.4 18.2 copy-start.2
  2088.7 18.2 copy-start.2
  2272.7 37.5 %copy-start.18 = (f32[8,3072]{1,0:T(8,128)S(1)}, f32[8,3072]{1,0:T(8,128)}, u32[]{:S(2)}) copy-start(f32[8,3072]{1,0:T(8,128)} %get-tuple-element.121) | copy-start | bytes 294916
  2272.7 37.5 %copy-start.21 = (f32[1,3072]{1,0:T(1,128)S(1)}, f32[1,3072]{1,0:T(1,128)}, u32[]{:S(2)}) copy-start(f32[1,3072]{1,0:T(1,128)} %get-tuple-element.137) | copy-start | bytes 36868
where the time goes:
time: 2480 us; the launch traced here: 2470 us
  matrix products  1070 us (43%)
  other arithmetic  432 us (17%)
  waiting for transfers between devices  404 us (16%)
  local copies, waits for them, and re-layouts  403 us (16%)
  blocking collectives  109 us (4%)
  starting transfers between devices  42.1 us (2%)
    dot_general x2, matrix products, project_in(): jnp.einsum('bsd,dn->bsn', modded, w_in, preferred_element_type=jnp.float32)  435 us
    dot_general x2, matrix products, project_out(): jnp.einsum('bsm,mn->bsn', mlp_act, w_out[model_dim:], preferred_element_t...  313 us
    all_to_all x2, waiting for transfers between devices, local_forward(): q_seq = lax.all_to_all(q_heads, 'sp', 2, 1, tiled=True)  167 us
    all_to_all x2, waiting for transfers between devices, local_forward(): k_seq = lax.all_to_all(k_heads, 'sp', 2, 1, tiled=True)  155 us
    reduce_sum x6, other arithmetic, per_block(): row_sum = jnp.sum(weights, axis=-1)  109 us
    all_to_all x1, blocking collectives, local_forward(): lax.all_to_all(attn_seq, 'sp', 1, 2, tiled=True)  109 us
    dot_general x6, matrix products, per_block(): jnp.einsum('bqhd,bkhd->bhqk', q_blk, keys_all, preferred_element_type=jnp...  105 us
    dot_general x6, matrix products, per_block(): jnp.einsum('bhqk,bkhd->bqhd', weights.astype(jnp.bfloat16), values_all, p...  103 us
  transfers between devices with their start and end apart: 7, of which 5 were waited for; matrix products, arithmetic and copies ran while one was open for 18% of the time, Pallas kernels for 0%

commit v1 on v0

v1 whole, which is shorter than its diff:
```python
import functools
import math
import jax
import jax.numpy as jnp
from jax import lax
from jax.experimental import pallas as pl
from jax.experimental.pallas import tpu as pltpu
from jax.sharding import PartitionSpec as P

HEAD = 128
HEADS = 24
D = 3072
MLP = 12288
QKV = 3 * D
NIN = QKV + MLP
ROWS = 192
ITEMS = 2
BLK = ITEMS * ROWS
HALF = 2 * BLK
GROUP = 4
LAYERS = 2
ROPE_SPLIT = (16, 56, 56)
ROPE_THETA = 10000.0
EPS = 1e-6
GELU_C = math.sqrt(2.0 / math.pi)
VMEM_LIMIT = 62 * 1024 * 1024
bf16 = jnp.bfloat16
f32 = jnp.float32


def dot(a, b):
    return jnp.dot(a, b, preferred_element_type=f32)


def layer_row(ref, layer, cs):
    both = ref[:, cs].astype(f32)
    return jnp.where(layer == 0, both[0:1], both[1:2])


def mod_cols(mod_ref, item, lo, hi):
    q = QKV // GROUP
    parts = []
    while lo < hi:
        end = min(hi, (lo // q + 1) * q)
        parts.append(mod_ref[lo // q, item:item + 1, lo % q:lo % q + end - lo])
        lo = end
    return parts[0] if len(parts) == 1 else jnp.concatenate(parts, axis=1)


def mod_body(s_ref, c_ref, w_ref, b_ref, o_ref):
    act = jax.nn.silu(c_ref[...].astype(f32)).astype(bf16)
    bias = layer_row(b_ref, pl.program_id(0), slice(None))
    o_ref[...] = (dot(act, w_ref[...]) + bias).astype(bf16)


def modulation(me, cond, w_mod, b_mod, tn=768):
    items = cond.shape[0]
    per = QKV // GROUP // tn
    return pl.pallas_call(
        mod_body,
        grid_spec=pltpu.PrefetchScalarGridSpec(
            num_scalar_prefetch=1,
            grid=(LAYERS, per),
            in_specs=[
                pl.BlockSpec((items, D), lambda l, n, s: (0, 0)),
                pl.BlockSpec((None, D, tn), lambda l, n, s: (l, 0, s[0] * per + n)),
                pl.BlockSpec((LAYERS, tn), lambda l, n, s: (0, s[0] * per + n)),
            ],
            out_specs=pl.BlockSpec((None, items, tn), lambda l, n, s: (l, 0, n)),
        ),
        out_shape=jax.ShapeDtypeStruct((LAYERS, items, QKV // GROUP), bf16),
        compiler_params=pltpu.CompilerParams(dimension_semantics=("arbitrary", "arbitrary"), vmem_limit_bytes=VMEM_LIMIT),
        cost_estimate=pl.CostEstimate(flops=2 * 16 * D * QKV // 2, bytes_accessed=D * QKV, transcendentals=items * D),
        name="modulation",
    )(me, cond, w_mod, b_mod)


def norm_rows(x_ref, u_ref, mod8_ref, base, ubase, sub, lc):
    def step(i, carry):
        r = pl.ds(pl.multiple_of(base + i * sub, sub), sub)
        ru = pl.ds(pl.multiple_of(ubase + i * sub, sub), sub)
        tot = jnp.zeros((sub, HEAD), f32)
        for c in range(D // lc):
            x = x_ref[r, c * lc:(c + 1) * lc].astype(f32)
            for j in range(lc // HEAD):
                tot += x[:, j * HEAD:(j + 1) * HEAD]
        mu = jnp.sum(tot, axis=-1, keepdims=True) * (1.0 / D)
        tot = jnp.zeros((sub, HEAD), f32)
        for c in range(D // lc):
            x = x_ref[r, c * lc:(c + 1) * lc].astype(f32)
            for j in range(lc // HEAD):
                d = x[:, j * HEAD:(j + 1) * HEAD] - mu
                tot += d * d
        rs = lax.rsqrt(jnp.sum(tot, axis=-1, keepdims=True) * (1.0 / D) + EPS)
        for c in range(D // lc):
            cs = slice(c * lc, (c + 1) * lc)
            x = x_ref[r, cs].astype(f32)
            xn = ((x - mu) * rs).reshape(sub // 8, 8, lc)
            y = xn * mod8_ref[1][None, :, cs] + mod8_ref[0][None, :, cs]
            u_ref[ru, cs] = y.reshape(sub, lc).astype(bf16)
        return carry

    lax.fori_loop(0, ROWS // sub, step, 0)


def swap_pairs(t):
    even = lax.broadcasted_iota(jnp.int32, t.shape, 1) % 2 == 0
    return jnp.where(even, pltpu.roll(t, HEAD - 1, 1), pltpu.roll(t, 1, 1))


def in_body(s_ref, x0_ref, x1_ref, mod_ref, w_ref, b_ref, t0_ref, t1_ref, qg_ref, kg_ref, *refs, tn, cw, n_after):
    qkv_ref, g_ref, u_ref, h_ref, mod8_ref, tab_ref = refs[n_after:]
    n = pl.program_id(0)
    nq = D // tn
    nt = NIN // tn

    @pl.when(n == 0)
    def _():
        for i, gain_ref in enumerate((qg_ref, kg_ref)):
            gain = jnp.broadcast_to(layer_row(gain_ref, s_ref[0], slice(None)), (8, HEAD))
            swapped = swap_pairs(gain)
            for blk, t_ref in enumerate((t0_ref, t1_ref)):
                for j, g in enumerate((gain, swapped)):
                    t = t_ref[j].reshape(ROWS // 8, 8, HEAD) * g[None]
                    tab_ref[i, j, blk * ROWS:(blk + 1) * ROWS] = t.reshape(ROWS, HEAD)
        for it in range(ITEMS):
            mod8_ref[0] = jnp.broadcast_to(mod_cols(mod_ref, it, 0, D).astype(f32), (8, D))
            mod8_ref[1] = jnp.broadcast_to(1.0 + mod_cols(mod_ref, it, D, 2 * D).astype(f32), (8, D))
            for blk, x_ref in enumerate((x0_ref, x1_ref)):
                norm_rows(x_ref, u_ref, mod8_ref, it * ROWS, (2 * blk + it) * ROWS, 96, 256)

    def mm(c):
        cs = slice(c * cw, (c + 1) * cw)
        acc = dot(u_ref[...], w_ref[:, cs]) + layer_row(b_ref, s_ref[0], cs)
        h_ref[:, cs] = acc.astype(bf16)

    def qk_post(c):
        i = jnp.clip((n - 1) // nq, 0, 1)
        tab = [
            jnp.concatenate([tab_ref[i, j, blk * ROWS:(blk + 1) * ROWS] for blk in (0, 0, 1, 1)], axis=0) for j in range(2)
        ]
        for hd in range(cw // HEAD):
            hs = slice(c * cw + hd * HEAD, c * cw + (hd + 1) * HEAD)
            hh = h_ref[:, hs].astype(f32)
            r = lax.rsqrt(jnp.sum(hh * hh, axis=-1, keepdims=True) * (1.0 / HEAD) + EPS)
            qkv_ref[:, hs] = ((hh * tab[0] + swap_pairs(hh) * tab[1]) * r).astype(bf16)

    def v_post(c):
        cs = slice(c * cw, (c + 1) * cw)
        qkv_ref[:, cs] = h_ref[:, cs]

    def g_post(c):
        cs = slice(c * cw, (c + 1) * cw)
        h = h_ref[:, cs].astype(f32)
        t = jnp.tanh(h * (GELU_C + (GELU_C * 0.044715) * (h * h)))
        hf = 0.5 * h
        g_ref[:, cs] = (hf + hf * t).astype(bf16)

    nc = tn // cw

    @pl.when(n <= 2 * nq)
    def _():
        for c in range(nc):
            qk_post(c)
            mm(c)

    @pl.when(jnp.logical_and(n > 2 * nq, n <= 3 * nq))
    def _():
        for c in range(nc):
            v_post(c)
            mm(c)

    @pl.when(jnp.logical_and(n > 3 * nq, n < nt))
    def _():
        for c in range(nc):
            g_post(c)
            mm(c)

    @pl.when(n == nt)
    def _():
        for c in range(nc):
            g_post(c)


def project_in(scalars, x0, x1, mod, w_in, b_in, tab, q_gain, k_gain, after, tn=1024, cw=256):
    nq = D // tn
    nt = NIN // tn
    one = pl.Buffered(1)
    cur = lambda n: jnp.minimum(n, nt - 1)
    prev = lambda n: jnp.maximum(n - 1, 0)
    return pl.pallas_call(
        functools.partial(in_body, tn=tn, cw=cw, n_after=len(after)),
        grid_spec=pltpu.PrefetchScalarGridSpec(
            num_scalar_prefetch=1,
            grid=(nt + 1,),
            in_specs=[
                pl.BlockSpec((BLK, D), lambda n, l: (0, 0), pipeline_mode=one),
                pl.BlockSpec((BLK, D), lambda n, l: (0, 0), pipeline_mode=one),
                pl.BlockSpec((None, GROUP, ITEMS, QKV // GROUP), lambda n, s: (s[0], 0, 0, 0), pipeline_mode=one),
                pl.BlockSpec((None, D, tn), lambda n, s: (s[0], 0, cur(n))),
                pl.BlockSpec((LAYERS, tn), lambda n, s: (0, cur(n))),
                pl.BlockSpec((2, None, ROWS, HEAD), lambda n, s: (0, s[1], 0, 0), pipeline_mode=one),
                pl.BlockSpec((2, None, ROWS, HEAD), lambda n, s: (0, s[2], 0, 0), pipeline_mode=one),
                pl.BlockSpec((LAYERS, HEAD), lambda n, s: (0, 0), pipeline_mode=one),
                pl.BlockSpec((LAYERS, HEAD), lambda n, s: (0, 0), pipeline_mode=one),
            ] + [pl.BlockSpec(memory_space=pl.ANY)] * len(after),
            out_specs=[
                pl.BlockSpec((HALF, tn), lambda n, l: (0, jnp.minimum(prev(n), 3 * nq - 1))),
                pl.BlockSpec((HALF, tn), lambda n, l: (0, jnp.maximum(prev(n) - 3 * nq, 0))),
            ],
            scratch_shapes=[
                pltpu.VMEM((HALF, D), bf16),
                pltpu.VMEM((HALF, tn), bf16),
                pltpu.VMEM((2, 8, D), f32),
                pltpu.VMEM((2, 2, BLK, HEAD), f32),
            ],
        ),
        out_shape=[jax.ShapeDtypeStruct((HALF, QKV), bf16), jax.ShapeDtypeStruct((HALF, MLP), bf16)],
        compiler_params=pltpu.CompilerParams(dimension_semantics=("arbitrary",), vmem_limit_bytes=VMEM_LIMIT),
        cost_estimate=pl.CostEstimate(
            flops=2 * HALF * D * NIN, bytes_accessed=2 * D * NIN + 2 * HALF * (NIN + D), transcendentals=HALF * MLP
        ),
        name="project_in",
    )(scalars, x0, x1, mod, w_in, b_in, tab, tab, q_gain, k_gain, *after)


def attn_body(*refs, nq, nh, qw):
    q_refs = refs[:nq]
    k_refs = refs[nq:nq + 2]
    v_refs = refs[nq + 2:nq + 4]
    o_refs = refs[nq + 4:2 * nq + 4]
    s_refs = refs[2 * nq + 4:]
    to_exp2 = HEAD ** -0.5 * math.log2(math.e)
    nqr = nq * 2 * ROWS
    nk = GROUP * ROWS
    kq = {}
    outs = {h: [] for h in range(nh)}

    def rows(rs, hs):
        return jnp.concatenate([r[b, :, hs] for r in rs for b in range(2)], axis=0)

    def load(h):
        hs = slice(h * HEAD, (h + 1) * HEAD)
        kq[h] = (rows(k_refs, hs), rows(q_refs, hs), rows(v_refs, hs).T)

    def front(h, a, slot):
        if h not in kq:
            load(h)
        k, q, _ = kq[h]
        m = None
        for j in range(0, nk, 256):
            s = lax.dot_general(k[j:j + 256], q[a:a + qw], (((1,), (1,)), ((), ())), preferred_element_type=f32)
            s_refs[slot][j:j + 256] = s
            mj = jnp.max(s.reshape(32, 8, qw), axis=0)
            m = mj if m is None else jnp.maximum(m, mj)
        return jnp.max(m, axis=0, keepdims=True)

    def back(h, a, slot, m):
        vt = kq[h][2]
        mc = jnp.broadcast_to(m * to_exp2, (8, qw))
        l = None
        ot = None
        for j in range(0, nk, 256):
            s = s_refs[slot][j:j + 256].reshape(32, 8, qw)
            p = jnp.exp2(s * to_exp2 - mc[None])
            lj = jnp.sum(p, axis=0)
            l = lj if l is None else l + lj
            oj = dot(vt[:, j:j + 256], p.reshape(256, qw).astype(bf16))
            ot = oj if ot is None else ot + oj
        l = jnp.sum(l, axis=0, keepdims=True)
        outs[h].append((ot * (1.0 / l)).T.astype(bf16))
        if a + qw >= nqr:
            o = jnp.concatenate(outs[h], axis=0)
            for j in range(nqr // ROWS):
                o_refs[j // 2][j % 2, :, h * HEAD:(h + 1) * HEAD] = o[j * ROWS:(j + 1) * ROWS]

    prev = None
    chunks = [(h, a) for h in range(nh) for a in range(0, nqr, qw)]
    for i, chunk in enumerate(chunks + [None]):
        this = None
        if chunk is not None:
            this = (*chunk, i % 2, front(*chunk, i % 2))
        if prev is not None:
            back(*prev)
        prev = this


def attention(qkvs, nh=12, qw=256):
    nq = len(qkvs)
    ng = HEADS // nh
    spec = lambda off: pl.BlockSpec((2, None, ROWS, nh * HEAD), lambda i, h: (0, i, 0, off * ng + h))
    views = [a.reshape(2, ITEMS, ROWS, QKV) for a in qkvs]
    pairs = ITEMS * HEADS * nq * 2 * ROWS * GROUP * ROWS
    outs = pl.pallas_call(
        functools.partial(attn_body, nq=nq, nh=nh, qw=qw),
        grid=(ITEMS, ng),
        in_specs=[spec(0)] * nq + [spec(1)] * 2 + [spec(2)] * 2,
        out_specs=[spec(0)] * nq,
        scratch_shapes=[pltpu.VMEM((GROUP * ROWS, qw), f32)] * 2,
        out_shape=[jax.ShapeDtypeStruct((2, ITEMS, ROWS, D), bf16)] * nq,
        compiler_params=pltpu.CompilerParams(dimension_semantics=("arbitrary", "arbitrary"), vmem_limit_bytes=VMEM_LIMIT),
        cost_estimate=pl.CostEstimate(flops=4 * pairs * HEAD, bytes_accessed=2 * 8 * HALF * D, transcendentals=pairs),
        name="attention",
    )(*views, *views, *views)
    return [o.reshape(HALF, D) for o in outs]


def out_body(s_ref, *refs, nb, tk, cw):
    o_ref, g_ref, w_ref, b_ref, mod_ref = refs[:5]
    x_refs = refs[5:5 + nb]
    y_refs = refs[5 + nb:5 + 2 * nb]
    acc_ref, x_buf, y_buf, isem, osem = refs[5 + 2 * nb:]
    k = pl.program_id(0)
    no = D // tk
    nk = (D + MLP) // tk

    def x_copy(b):
        return pltpu.make_async_copy(x_refs[b], x_buf.at[pl.ds(b * BLK, BLK)], isem.at[b])

    def cols(c):
        return slice(c * cw, (c + 1) * cw)

    @pl.when(k == 0)
    def _():
        for b in range(nb):
            x_copy(b).start()
        for c in range(D // cw):
            acc_ref[:, cols(c)] = dot(o_ref[...], w_ref[:, cols(c)])

    @pl.when(jnp.logical_and(k > 0, k < no))
    def _():
        for c in range(D // cw):
            acc_ref[:, cols(c)] += dot(o_ref[...], w_ref[:, cols(c)])

    @pl.when(jnp.logical_and(k >= no, k < nk - 1))
    def _():
        for c in range(D // cw):
            acc_ref[:, cols(c)] += dot(g_ref[...], w_ref[:, cols(c)])

    @pl.when(k == nk - 1)
    def _():
        for b in range(nb):
            x_copy(b).wait()
        for c in range(D // cw):
            cs = cols(c)
            y = acc_ref[:, cs] + dot(g_ref[...], w_ref[:, cs])
            y = (y + layer_row(b_ref, s_ref[0], cs)).astype(bf16).astype(f32)
            for b in range(nb):
                for it in range(ITEMS):
                    rs = slice(b * BLK + it * ROWS, b * BLK + (it + 1) * ROWS)
                    gate = mod_cols(mod_ref, it, 2 * D + c * cw, 2 * D + (c + 1) * cw).astype(f32)
                    y_buf[rs, cs] = (x_buf[rs, cs].astype(f32) + gate * y[rs]).astype(bf16)
            for b in range(nb):
                pltpu.make_async_copy(
                    y_buf.at[pl.ds(b * BLK, BLK), pl.ds(c * cw, cw)], y_refs[b].at[:, pl.ds(c * cw, cw)], osem.at[b]
                ).start()
        for b in range(nb):
            pltpu.make_async_copy(y_buf.at[pl.ds(b * BLK, BLK)], y_refs[b], osem.at[b]).wait()


def project_out(layer, o, g, w_out, b_out, mod, xs, rb, tk=1024, cw=512):
    nb = len(xs)
    r = BLK * nb
    no = D // tk
    nk = (D + MLP) // tk
    one = pl.Buffered(1)
    hbm = pl.BlockSpec(memory_space=pl.ANY)
    return pl.pallas_call(
        functools.partial(out_body, nb=nb, tk=tk, cw=cw),
        grid_spec=pltpu.PrefetchScalarGridSpec(
            num_scalar_prefetch=1,
            grid=(nk,),
            in_specs=[
                pl.BlockSpec((r, tk), lambda k, l: (l[1], jnp.minimum(k, no - 1))),
                pl.BlockSpec((r, tk), lambda k, l: (l[1], jnp.maximum(k - no, 0))),
                pl.BlockSpec((None, tk, D), lambda k, l: (l[0], k, 0)),
                pl.BlockSpec((LAYERS, D), lambda k, l: (0, 0), pipeline_mode=one),
                pl.BlockSpec((None, GROUP, ITEMS, QKV // GROUP), lambda k, l: (l[0], 0, 0, 0), pipeline_mode=one),
            ] + [hbm] * nb,
            out_specs=[hbm] * nb,
            scratch_shapes=[
                pltpu.VMEM((r, D), f32),
                pltpu.VMEM((r, D), bf16),
                pltpu.VMEM((r, D), bf16),
                pltpu.SemaphoreType.DMA((nb,)),
                pltpu.SemaphoreType.DMA((nb,)),
            ],
        ),
        out_shape=[jax.ShapeDtypeStruct((BLK, D), bf16)] * nb,
        compiler_params=pltpu.CompilerParams(dimension_semantics=("arbitrary",), vmem_limit_bytes=VMEM_LIMIT),
        cost_estimate=pl.CostEstimate(
            flops=2 * r * D * (D + MLP), bytes_accessed=2 * D * (D + MLP) + 2 * r * (3 * D + MLP), transcendentals=0
        ),
        name="project_out",
    )(jnp.array([layer, rb], jnp.int32), o, g, w_out, b_out, mod, *xs)


def place_body(s_ref, *refs):
    o_ref = refs[GROUP]
    for k in range(GROUP):
        @pl.when(pl.program_id(0) == k)
        def _(k=k):
            o_ref[...] = refs[k][...].reshape(o_ref.shape)


def place(me, blocks):
    return pl.pallas_call(
        place_body,
        grid_spec=pltpu.PrefetchScalarGridSpec(
            num_scalar_prefetch=1,
            grid=(GROUP,),
            in_specs=[pl.BlockSpec((BLK, D), lambda k, s: (0, 0), pipeline_mode=pl.Buffered(1))] * GROUP,
            out_specs=pl.BlockSpec((ITEMS, ROWS, D), lambda k, s: (jnp.bitwise_xor(s[0], k), 0, 0)),
        ),
        out_shape=jax.ShapeDtypeStruct((GROUP * ITEMS, ROWS, D), bf16),
        compiler_params=pltpu.CompilerParams(dimension_semantics=("arbitrary",), vmem_limit_bytes=VMEM_LIMIT),
        cost_estimate=pl.CostEstimate(flops=0, bytes_accessed=4 * GROUP * BLK * D, transcendentals=0),
        name="place",
    )(me, *blocks)


def rope_table(pos):
    lane = jnp.arange(HEAD, dtype=jnp.int32)
    pair = lane // 2
    ang = None
    start = 0
    for column, dim in enumerate(ROPE_SPLIT):
        freq = 1.0 / (ROPE_THETA ** ((2 * pair - start).astype(f32) / dim))
        part = pos[:, :, column:column + 1].astype(f32) * freq
        ang = part if ang is None else jnp.where(lane >= start, part, ang)
        start += dim
    return jnp.stack([jnp.cos(ang), jnp.where(lane % 2 == 0, -1.0, 1.0) * jnp.sin(ang)])


def solution(mesh):
    def local(hidden, cond, pos_ids, w_mod, b_mod, w_in, b_in, q_gain, k_gain, w_out, b_out):
        me = lax.axis_index("sp").astype(jnp.int32)
        me1 = me.reshape(1)
        source = [jnp.bitwise_xor(me, k) for k in range(GROUP)]
        swap = lambda a, k: lax.ppermute(a, "sp", [(i, i ^ k) for i in range(GROUP)])
        piece = lambda k: lax.dynamic_slice_in_dim(hidden, ITEMS * source[k], ITEMS, axis=0).reshape(BLK, D)

        x = [piece(0), swap(piece(1), 1)]
        tab = rope_table(lax.all_gather(pos_ids, "sp"))
        part = modulation(me1, cond, w_mod, b_mod).reshape(LAYERS, GROUP, ITEMS, QKV // GROUP)
        mod = lax.all_to_all(part, "sp", 1, 1)
        far = [piece(2), piece(3)]
        far, mod, x, tab = lax.optimization_barrier((far, mod, x, tab))
        x += [swap(far[0], 2), swap(far[1], 3)]

        for layer in range(LAYERS):
            halves = []
            for i in range(2):
                scalars = jnp.stack([jnp.int32(layer), source[2 * i], source[2 * i + 1]])
                after = [h[0] for h in halves] if halves else [x[0]]
                halves.append(
                    project_in(scalars, x[2 * i], x[2 * i + 1], mod, w_in, b_in, tab, q_gain, k_gain, [after[0]])
                )
            att = attention([h[0] for h in halves])
            if layer < LAYERS - 1:
                x = [
                    y
                    for i in range(2)
                    for y in project_out(layer, att[i], halves[i][1], w_out, b_out, mod, x[2 * i:2 * i + 2], 0)
                ]
        out = {}
        for k in (2, 3, 1, 0):
            i = k // 2
            out[k] = project_out(layer, att[i], halves[i][1], w_out, b_out, mod, [x[k]], k % 2, tk=1536)[0]
            if k:
                out[k] = swap(out[k], k)
        return place(me1, [out[k] for k in range(GROUP)])

    rows = P("dp", "sp", None)
    rep = P()
    specs = (rows, P("dp", None), P("sp", None)) + (rep,) * 8
    return jax.shard_map(local, mesh=mesh, in_specs=specs, out_specs=rows, check_vma=False)
```

time: 2480 us -> 1020 us (0.41)
  matrix products: 1070 us -> 0 us
  Pallas kernels: 0 us -> 986 us
  other arithmetic: 432 us -> 5.57 us
  waiting for transfers between devices: 404 us -> 0.02 us
  local copies, waits for them, and re-layouts: 403 us -> 11.2 us
  blocking collectives: 109 us -> 5.54 us
  starting transfers between devices: 42.1 us -> 8.53 us
    dot_general x20 -> x0, matrix products: 1070 us -> none  [the longest x2 435 us: project_in(): jnp.einsum('bsd,dn->bsn', modded, w_in, preferred_element_type=jnp.float32)]
    pallas_call x0 -> x14, Pallas kernels: none -> 986 us  [the longest x4 527 us: project_in(): pl.pallas_call(functools.partial(in_body, tn=tn, cw=cw, n_after=len(after...]
    all_to_all x7 -> x1, waiting for transfers between devices: 404 us -> 0.01 us  [local(): mod = lax.all_to_all(part, 'sp', 1, 1)]
    convert_element_type x12 -> x0, local copies, waits for them, and re-layouts: 166 us -> none  [the longest x2 49.9 us: qkv_heads(): proj_in[..., model_dim:2 * model_dim].reshape(head_shape)]
    reduce_sum x13 -> x0, other arithmetic: 160 us -> none  [the longest x6 109 us: per_block(): row_sum = jnp.sum(weights, axis=-1)]
    all_to_all x1 -> x0, blocking collectives: 109 us -> none  [local_forward(): lax.all_to_all(attn_seq, 'sp', 1, 2, tiled=True)]
    another operation x6 -> x3, other arithmetic: 97.5 us -> 2.25 us  [the longest x2 1.31 us: local(): scalars = jnp.stack([jnp.int32(layer), source[2 * i], source[2 * i + 1]])]
    mul x10 -> x0, other arithmetic: 93.9 us -> none  [the longest x4 56.8 us: rms_norm(): return tensor * lax.rsqrt(sq_mean + NORM_EPS) * gain.astype(jnp.float32)]
  transfers between devices with their start and end apart: 7 -> 7, of which waited for: 5 -> 0; matrix products, arithmetic and copies ran while one was open for 18% -> 1% of each run, Pallas kernels for 0% -> 28%
where the time goes in v1:
time: 1020 us
  Pallas kernels  986 us (97%)
  local copies, waits for them, and re-layouts  11.2 us (1%)
    pallas_call x4, Pallas kernels, project_in(): pl.pallas_call(functools.partial(in_body, tn=tn, cw=cw, n_after=len(after...  527 us
    pallas_call x6, Pallas kernels, project_out(): pl.pallas_call(functools.partial(out_body, nb=nb, tk=tk, cw=cw), grid_spe...  350 us
    pallas_call x2, Pallas kernels, attention(): pl.pallas_call(functools.partial(attn_body, nq=nq, nh=nh, qw=qw), grid=(I...  89.7 us
  transfers between devices with their start and end apart: 7, of which 0 were waited for; matrix products, arithmetic and copies ran while one was open for 1% of the time, Pallas kernels for 28%

profile of v1, /device:TPU:0, one launch (start us, length us, event | category | flops | bytes accessed | tf_op | source)
XLA Modules:
  0.0 1017.2 jit_solution(17655662642799111630)
XLA Ops:
  0.0 7.8 constant_dynamic-slice_fusion
  7.8 0.7 collective-permute-start
  8.6 0.0 copy-start
  8.6 11.8 %modulation.1 = bf16[2,8,2304]{2,1,0:T(8,128)(2,1)} custom-call(s32[1]{0:T(128)} %bitcast.s_ref, bf16[8,3072]{1,0:T(8,128)(2,1)} %c_ref.1, bf16[2,3072,9216]{2,1,0:T(8,128)(2,1)} %w_ref.5, bf16[2,9216]{1,0:T(2,128)(2,1)} %b_ref.5), custom_call_target="tpu_custom_call" | custom-call | flops 452984832 | bytes 28311552 | tf_op jit(solution)/shard_map/modulation/pallas_call | solution.py:59
  20.3 0.9 reshape.112
  21.2 0.7 copy.18
  21.9 3.9 all-to-all-start
  25.8 0.0 copy-done
  25.8 5.5 all-gather.1
  31.4 0.7 fusion.1
  32.1 3.3 fusion
  35.4 0.9 pad_maximum_fusion.t0_ref.t1_ref
  36.3 0.7 fusion.2
  37.0 0.0 all-to-all-done
  37.0 0.0 collective-permute-done.x1_ref.refs_6_
  37.0 0.7 copy.19.mod_ref.refs_4_
  37.7 1.6 collective-permute-start.1
  39.3 0.1 collective-permute-start.2
  39.4 131.5 %project_in.4 = (bf16[768,9216]{1,0:T(8,128)(2,1)}, bf16[768,12288]{1,0:T(8,128)(2,1)}) custom-call(s32[3]{0:T(128)} %get-tuple-element.58.s_ref, bf16[384,3072]{1,0:T(8,128)(2,1)} %bitcast.40, bf16[384,3072]{1,0:T(8,128)(2,1)} %collective-permute-done.x1_ref.refs_6_, bf16[2,4,2,2304]{3,2,1,0:T(2,128)(2,1)} %copy.19.mod_ref.refs_4_, ...), custom_call_target="tpu_custom_call" | custom-call | flops 101468602368 | bytes 169869312 | tf_op jit(solution)/shard_map/project_in/pallas_call | solution.py:191
  170.9 0.0 collective-permute-done.1.x0_ref.refs_5_
  170.9 0.0 collective-permute-done.2.x1_ref.refs_6_
  170.9 131.9 %project_in.5 = (bf16[768,9216]{1,0:T(8,128)(2,1)}, bf16[768,12288]{1,0:T(8,128)(2,1)}) custom-call(s32[3]{0:T(128)} %get-tuple-element.62.s_ref, bf16[384,3072]{1,0:T(8,128)(2,1)} %collective-permute-done.1.x0_ref.refs_5_, bf16[384,3072]{1,0:T(8,128)(2,1)} %collective-permute-done.2.x1_ref.refs_6_, bf16[2,4,2,2304]{3,2,1,0:T(2,128)(2,1)} %copy.19.mod_ref.refs_4_, ...), custom_call_target="tpu_custom_call" | custom-call | flops 101468602368 | bytes 169869312 | tf_op jit(solution)/shard_map/project_in/pallas_call | solution.py:191
  302.9 44.8 %attention.2 = (bf16[2,2,192,3072]{3,2,1,0:T(8,128)(2,1)}, bf16[2,2,192,3072]{3,2,1,0:T(8,128)(2,1)}) custom-call(bf16[2,2,192,9216]{3,2,1,0:T(8,128)(2,1)} %bitcast.27, bf16[2,2,192,9216]{3,2,1,0:T(8,128)(2,1)} %bitcast.33, bf16[2,2,192,9216]{3,2,1,0:T(8,128)(2,1)} %bitcast.28, bf16[2,2,192,9216]{3,2,1,0:T(8,128)(2,1)} %bitcast.34, ...), custom_call_target="tpu_custom_call" | custom-call | flops 14495514624 | bytes 37748736 | tf_op jit(solution)/shard_map/attention/pallas_call | solution.py:294
  347.7 0.6 call_exported.0.s_ref
  348.3 83.3 %project_out.6 = (bf16[384,3072]{1,0:T(8,128)(2,1)}, bf16[384,3072]{1,0:T(8,128)(2,1)}) custom-call(s32[2]{0:T(128)} %call_exported.0.s_ref, bf16[768,3072]{1,0:T(8,128)(2,1)} %bitcast.46, bf16[768,12288]{1,0:T(8,128)(2,1)} %get-tuple-element.36.refs_1_, bf16[2,15360,3072]{2,1,0:T(8,128)(2,1)} %refs_2_.11, bf16[2,3072]{1,0:T(2,128)(2,1)} %refs_3_.11, ...), custom_call_target="tpu_custom_call" | custom-call | flops 72477573120 | bytes 127401984 | tf_op jit(solution)/shard_map/project_out/pallas_call | solution.py:368
  431.6 131.8 %project_in.6 = (bf16[768,9216]{1,0:T(8,128)(2,1)}, bf16[768,12288]{1,0:T(8,128)(2,1)}) custom-call(s32[3]{0:T(128)} %get-tuple-element.59.s_ref, bf16[384,3072]{1,0:T(8,128)(2,1)} %get-tuple-element.37.x0_ref.refs_0_.refs_5_, bf16[384,3072]{1,0:T(8,128)(2,1)} %get-tuple-element.38.x1_ref.refs_5_, bf16[2,4,2,2304]{3,2,1,0:T(2,128)(2,1)} %copy.19.mod_ref.refs_4_, ...), custom_call_target="tpu_custom_call" | custom-call | flops 101468602368 | bytes 169869312 | tf_op jit(solution)/shard_map/project_in/pallas_call | solution.py:191
  563.4 82.9 %project_out.7 = (bf16[384,3072]{1,0:T(8,128)(2,1)}, bf16[384,3072]{1,0:T(8,128)(2,1)}) custom-call(s32[2]{0:T(128)} %call_exported.0.s_ref, bf16[768,3072]{1,0:T(8,128)(2,1)} %bitcast.45, bf16[768,12288]{1,0:T(8,128)(2,1)} %get-tuple-element.41.refs_1_, bf16[2,15360,3072]{2,1,0:T(8,128)(2,1)} %refs_2_.11, bf16[2,3072]{1,0:T(2,128)(2,1)} %refs_3_.11, ...), custom_call_target="tpu_custom_call" | custom-call | flops 72477573120 | bytes 127401984 | tf_op jit(solution)/shard_map/project_out/pallas_call | solution.py:368
  646.4 131.5 %project_in.7 = (bf16[768,9216]{1,0:T(8,128)(2,1)}, bf16[768,12288]{1,0:T(8,128)(2,1)}) custom-call(s32[3]{0:T(128)} %get-tuple-element.63.s_ref, bf16[384,3072]{1,0:T(8,128)(2,1)} %get-tuple-element.42.x0_ref.refs_5_, bf16[384,3072]{1,0:T(8,128)(2,1)} %get-tuple-element.43.x1_ref.refs_5_, bf16[2,4,2,2304]{3,2,1,0:T(2,128)(2,1)} %copy.19.mod_ref.refs_4_, ...), custom_call_target="tpu_custom_call" | custom-call | flops 101468602368 | bytes 169869312 | tf_op jit(solution)/shard_map/project_in/pallas_call | solution.py:191
  777.9 44.9 %attention.3 = (bf16[2,2,192,3072]{3,2,1,0:T(8,128)(2,1)}, bf16[2,2,192,3072]{3,2,1,0:T(8,128)(2,1)}) custom-call(bf16[2,2,192,9216]{3,2,1,0:T(8,128)(2,1)} %bitcast.24, bf16[2,2,192,9216]{3,2,1,0:T(8,128)(2,1)} %bitcast.30, bf16[2,2,192,9216]{3,2,1,0:T(8,128)(2,1)} %bitcast.25, bf16[2,2,192,9216]{3,2,1,0:T(8,128)(2,1)} %bitcast.31, ...), custom_call_target="tpu_custom_call" | custom-call | flops 14495514624 | bytes 37748736 | tf_op jit(solution)/shard_map/attention/pallas_call | solution.py:294
  822.7 0.5 call_exported.1.s_ref
  823.2 46.0 %project_out.11 = bf16[384,3072]{1,0:T(8,128)(2,1)} custom-call(s32[2]{0:T(128)} %call_exported.1.s_ref, bf16[768,3072]{1,0:T(8,128)(2,1)} %bitcast.38, bf16[768,12288]{1,0:T(8,128)(2,1)} %get-tuple-element.48.refs_1_, bf16[2,15360,3072]{2,1,0:T(8,128)(2,1)} %refs_2_.11, bf16[2,3072]{1,0:T(2,128)(2,1)} %refs_3_.11, ...), custom_call_target="tpu_custom_call" | custom-call | flops 36238786560 | bytes 110886912 | tf_op jit(solution)/shard_map/project_out/pallas_call | solution.py:368
  869.3 1.7 collective-permute-start.5
  871.0 45.8 %project_out.10 = bf16[384,3072]{1,0:T(8,128)(2,1)} custom-call(s32[2]{0:T(128)} %constant.78.clone.s_ref, bf16[768,3072]{1,0:T(8,128)(2,1)} %bitcast.39, bf16[768,12288]{1,0:T(8,128)(2,1)} %get-tuple-element.48.refs_1_, bf16[2,15360,3072]{2,1,0:T(8,128)(2,1)} %refs_2_.11, bf16[2,3072]{1,0:T(2,128)(2,1)} %refs_3_.11, ...), custom_call_target="tpu_custom_call" | custom-call | flops 36238786560 | bytes 110886912 | tf_op jit(solution)/shard_map/project_out/pallas_call | solution.py:368
  916.8 0.4 collective-permute-start.4
  917.2 45.8 %project_out.9 = bf16[384,3072]{1,0:T(8,128)(2,1)} custom-call(s32[2]{0:T(128)} %call_exported.1.s_ref, bf16[768,3072]{1,0:T(8,128)(2,1)} %bitcast.36, bf16[768,12288]{1,0:T(8,128)(2,1)} %get-tuple-element.46.refs_1_, bf16[2,15360,3072]{2,1,0:T(8,128)(2,1)} %refs_2_.11, bf16[2,3072]{1,0:T(2,128)(2,1)} %refs_3_.11, ...), custom_call_target="tpu_custom_call" | custom-call | flops 36238786560 | bytes 110886912 | tf_op jit(solution)/shard_map/project_out/pallas_call | solution.py:368
  963.1 0.0 collective-permute-start.3
  963.1 45.9 %project_out.8.refs_0_ = bf16[384,3072]{1,0:T(8,128)(2,1)} custom-call(s32[2]{0:T(128)} %constant.78.clone.s_ref, bf16[768,3072]{1,0:T(8,128)(2,1)} %bitcast.37, bf16[768,12288]{1,0:T(8,128)(2,1)} %get-tuple-element.46.refs_1_, bf16[2,15360,3072]{2,1,0:T(8,128)(2,1)} %refs_2_.11, bf16[2,3072]{1,0:T(2,128)(2,1)} %refs_3_.11, ...), custom_call_target="tpu_custom_call" | custom-call | flops 36238786560 | bytes 110886912 | tf_op jit(solution)/shard_map/project_out/pallas_call | solution.py:368
  1009.0 0.0 collective-permute-done.5.refs_3_
  1009.1 0.0 collective-permute-done.4.refs_2_
  1009.1 0.0 collective-permute-done.3.refs_1_
  1009.1 7.7 place.1
  (6 shorter events, 0.0 us)
Async XLA Ops:
  7.8 29.2 %collective-permute-start = (bf16[384,3072]{1,0:T(8,128)(2,1)}, bf16[384,3072]{1,0:T(8,128)(2,1)}, u32[]{:S(2)}, u32[]{:S(2)}) collective-permute-start(bf16[384,3072]{1,0:T(8,128)(2,1)} %bitcast.5), channel_id=1, source_target_pairs={{0,1},{1,0},{2,3},{3,2},{4,5},{5,4},{6,7},{7,6},{8,9},{9,8},{10,11... | collective-permute-start | bytes 7077896 | tf_op jit(solution)/shard_map/ppermute | solution.py:440
  8.6 17.3 %copy-start = (s32[192,3]{0,1:T(4,128)S(1)}, s32[192,3]{0,1:T(4,128)}, u32[]{:S(2)}) copy-start(s32[192,3]{0,1:T(4,128)} %param.19) | copy-start | bytes 6916
  21.9 15.1 %all-to-all-start = ((bf16[2,4,2,2304]{3,2,0,1:T(2,128)(2,1)}), bf16[2,4,2,2304]{3,2,0,1:T(2,128)(2,1)S(1)}, u32[]{:S(2)}, u32[]{:S(2)}) async-start(bf16[2,4,2,2304]{3,2,0,1:T(2,128)(2,1)} %copy.18), calls=%async_computation | async-start | bytes 147456 | tf_op jit(solution)/shard_map/all_to_all | solution.py:446
  37.7 133.2 %collective-permute-start.1 = (bf16[384,3072]{1,0:T(8,128)(2,1)}, bf16[384,3072]{1,0:T(8,128)(2,1)}, u32[]{:S(2)}, u32[]{:S(2)}) collective-permute-start(bf16[384,3072]{1,0:T(8,128)(2,1)} %bitcast.2), channel_id=1, source_target_pairs={{0,2},{1,3},{2,0},{3,1},{4,6},{5,7},{6,4},{7,5},{8,10},{9,11},{10,... | collective-permute-start | bytes 7077896 | tf_op jit(solution)/shard_map/ppermute | solution.py:440
  39.3 131.6 %collective-permute-start.2 = (bf16[384,3072]{1,0:T(8,128)(2,1)}, bf16[384,3072]{1,0:T(8,128)(2,1)}, u32[]{:S(2)}, u32[]{:S(2)}) collective-permute-start(bf16[384,3072]{1,0:T(8,128)(2,1)} %bitcast.3), channel_id=1, source_target_pairs={{0,3},{1,2},{2,1},{3,0},{4,7},{5,6},{6,5},{7,4},{8,11},{9,10},{10,... | collective-permute-start | bytes 7077896 | tf_op jit(solution)/shard_map/ppermute | solution.py:440
  869.3 139.8 %collective-permute-start.5 = (bf16[384,3072]{1,0:T(8,128)(2,1)}, bf16[384,3072]{1,0:T(8,128)(2,1)}, u32[]{:S(2)}, u32[]{:S(2)}) collective-permute-start(bf16[384,3072]{1,0:T(8,128)(2,1)} %project_out.11), channel_id=1, source_target_pairs={{0,3},{1,2},{2,1},{3,0},{4,7},{5,6},{6,5},{7,4},{8,11},{9,10},{10,... | collective-permute-start | bytes 7077896 | tf_op jit(solution)/shard_map/ppermute | solution.py:440
  916.8 92.2 %collective-permute-start.4 = (bf16[384,3072]{1,0:T(8,128)(2,1)}, bf16[384,3072]{1,0:T(8,128)(2,1)}, u32[]{:S(2)}, u32[]{:S(2)}) collective-permute-start(bf16[384,3072]{1,0:T(8,128)(2,1)} %project_out.10), channel_id=1, source_target_pairs={{0,2},{1,3},{2,0},{3,1},{4,6},{5,7},{6,4},{7,5},{8,10},{9,11},{10,... | collective-permute-start | bytes 7077896 | tf_op jit(solution)/shard_map/ppermute | solution.py:440
  963.1 46.0 %collective-permute-start.3 = (bf16[384,3072]{1,0:T(8,128)(2,1)}, bf16[384,3072]{1,0:T(8,128)(2,1)}, u32[]{:S(2)}, u32[]{:S(2)}) collective-permute-start(bf16[384,3072]{1,0:T(8,128)(2,1)} %project_out.9), channel_id=1, source_target_pairs={{0,1},{1,0},{2,3},{3,2},{4,5},{5,4},{6,7},{7,6},{8,9},{9,8},{10,11... | collective-permute-start | bytes 7077896 | tf_op jit(solution)/shard_map/ppermute | solution.py:440
